TPU v7x, 32 devices: a whole 2x2x4 slice. The times are simulated.
32 devices in a mesh: sx: 4 (over x, core), sy: 4 (over z), dp: 2 (over y).
Axes of the slice: x: 2, y: 2, z: 4, core: 2. Of those that a mesh axis runs over, the one named last changes fastest.
Arguments:
- tokens: bfloat16 [2, 8192, 1280], P('dp', ('sx', 'sy')), may hold values from -6 to 6
- lengths: int32 [2, 64], P('dp'), may hold values from 1 to 512, 8192 in all within a row
- ln_gain: float32 [1280], replicated, may hold values from 0.1 to 1.9
- w_qkv: bfloat16 [1280, 3840], P('dp'), may hold values from -4 to 4, as said below
- w_out: bfloat16 [1280, 1280], P('dp'), may hold values from -0.15625 to 0.15625
Outputs:
- hidden: bfloat16 [2, 8192, 1280], P('dp', ('sx', 'sy'))
- pooled: float32 [2, 64, 1280], P('dp')
Inputs may be any that keep to these rules, and one draw needn't show every extreme that they name: The 64 lengths of a row sum to 8192; images are packed end to end in order. `w_qkv`: columns are queries, then keys, then values, each of 16 heads of 80 columns.
All inputs are finite; a program needn't handle non-finite values.
Results may differ from a plain program's by a relative error of at most 0.0051.
Values may be sent and summed in bfloat16 or wider, within the bound.
A program may use at most 128 MiB of HBM per device.

v0:
```python
import jax
import jax.numpy as jnp
from jax import lax
from jax.sharding import PartitionSpec as P

HEADS = 16
MAXLEN = 512


def with_halo(block, sides, width):
    for axis, dim in sides:
        count = lax.axis_size(axis)
        forward = [(i, i + 1) for i in range(count - 1)]
        backward = [(target, source) for source, target in forward]
        low = lax.ppermute(
            lax.slice_in_dim(block, block.shape[dim] - width, None, axis=dim), axis, forward
        )
        high = lax.ppermute(lax.slice_in_dim(block, 0, width, axis=dim), axis, backward)
        block = jnp.concatenate([low, block, high], axis=dim)
    return block


def image_ids(lengths, positions, total):
    offsets = jnp.cumsum(lengths) - lengths
    counted = jnp.sum((offsets[None, :] <= positions[:, None]).astype(jnp.int32), axis=1) - 1
    inside = (positions >= 0) & (positions < total)
    return jnp.where(inside, counted, -1)


def normalize(rows, ln_gain):
    values = rows.astype(jnp.float32)
    center = values - jnp.mean(values, axis=-1, keepdims=True)
    spread = jnp.mean(center * center, axis=-1, keepdims=True)
    return (center * lax.rsqrt(spread + 1e-05) * ln_gain).astype(jnp.bfloat16)


def attend(queries, keys, values, q_ids, k_ids):
    length = queries.shape[0]
    heads = queries.shape[1]
    block = min(512, length)
    scale = queries.shape[2] ** (-0.5)

    def one_block(index):
        allowed = q_ids[:, None] == k_ids[None, :]

        def one_head(head):
            q_head = lax.dynamic_index_in_dim(queries, head, 1, keepdims=False)
            k_head = lax.dynamic_index_in_dim(keys, head, 1, keepdims=False)
            v_head = lax.dynamic_index_in_dim(values, head, 1, keepdims=False)
            scores = jnp.dot(q_head, k_head.T, preferred_element_type=jnp.float32) * scale
            scores = jnp.where(allowed, scores, -1e30)
            top = jnp.max(scores, axis=1, keepdims=True)
            weights = jnp.exp(scores - top)
            probs = (weights / jnp.sum(weights, axis=1, keepdims=True)).astype(jnp.bfloat16)
            return jnp.dot(probs, v_head, preferred_element_type=jnp.float32).astype(jnp.bfloat16)

        outcome = lax.map(one_head, jnp.arange(heads, dtype=jnp.int32))
        return jnp.transpose(outcome, (1, 0, 2))

    blocks = lax.map(one_block, jnp.arange(length // block, dtype=jnp.int32))
    return blocks.reshape(length, heads, -1)


def shards(tokens, lengths, ln_gain, w_qkv, w_out):
    qkv_full, out_full = (
        lax.all_gather(w_qkv, "dp", axis=0, tiled=True),
        lax.all_gather(w_out, "dp", axis=0, tiled=True),
    )
    count_rows = tokens.shape[0]
    local = tokens.shape[1]
    width = tokens.shape[2]
    size = width // HEADS
    images = lengths.shape[1]
    count_x = lax.axis_size("sx")
    count_y = lax.axis_size("sy")
    total = local * count_x * count_y
    shard = lax.axis_index("sx") * count_y + lax.axis_index("sy")
    own_positions = shard * local + jnp.arange(local, dtype=jnp.int32)
    own_list = [image_ids(lengths[0], own_positions, total)]
    normed = normalize(tokens, ln_gain)
    qkv = jnp.dot(
        normed.reshape(count_rows * local, width), qkv_full, preferred_element_type=jnp.float32
    )
    qkv = qkv.astype(jnp.bfloat16).reshape(count_rows, local, 3 * width)
    pieces = qkv.reshape(count_rows, local, 3, HEADS, size)
    keyvals = with_halo(pieces[:, :, 1:3], ((("sx", "sy"), 1),), MAXLEN)
    k_pos = shard * local - MAXLEN + jnp.arange(local + 2 * MAXLEN, dtype=jnp.int32)
    rowidx = 0
    k_ids = image_ids(lengths[rowidx], k_pos, total)
    outcomes = [
        attend(
            pieces[rowidx, :, 0],
            keyvals[rowidx, :, 0],
            keyvals[rowidx, :, 1],
            own_list[rowidx],
            k_ids,
        )
    ]
    context = jnp.stack(outcomes, axis=0).reshape(count_rows * local, width)
    mixed = jnp.dot(context, out_full, preferred_element_type=jnp.float32).reshape(
        count_rows, local, width
    )
    hidden = (tokens.astype(jnp.float32) + mixed).astype(jnp.bfloat16)
    labels = jnp.arange(images, dtype=jnp.int32)
    rowidx = 0
    onehot = (labels[:, None] == own_list[rowidx][None, :]).astype(jnp.bfloat16)
    parts_list = [jnp.dot(onehot, hidden[rowidx], preferred_element_type=jnp.float32)]
    terms = jnp.stack(parts_list, axis=0)
    sums = lax.psum(terms, ("sx", "sy"))
    pooled = sums / lengths.astype(jnp.float32)[:, :, None]
    return (hidden, pooled)


def solution(mesh):
    in_specs = (P("dp", ("sx", "sy"), None), P("dp", None), P(), P("dp", None), P("dp", None))
    out_specs = (P("dp", ("sx", "sy"), None), P("dp", None, None))
    return jax.shard_map(shards, mesh=mesh, in_specs=in_specs, out_specs=out_specs, check_vma=False)
```

profile of v0, /device:TPU:8, one launch (start us, length us, event | category | flops | bytes accessed | tf_op | source)
XLA Modules:
  0.0 491.2 jit_solution(5797661446178218919)
XLA Ops:
  9.2 123.8 %all-gather.3.cloned.1.call-done = bf16[1280,3840]{1,0:T(8,128)(2,1)} async-done(((bf16[640,3840]{1,0:T(8,128)(2,1)}), bf16[1280,3840]{1,0:T(8,128)(2,1)}) %all-gather.3.cloned.1.call-update) | async-done | bytes 9830416 | tf_op jit(solution)/shard_map/all_gather | solution.py:66
  133.0 10.9 %convolution_convert_fusion = bf16[512,3840]{1,0:T(8,128)(2,1)} fusion(bf16[1280,3840]{1,0:T(8,128)(2,1)} %all-gather.3.cloned.1.call-done, bf16[1,512,1280]{2,1,0:T(8,128)(2,1)S(1)} %copy-done, f32[1280]{0:T(1024)S(1)} %copy-done.4, f32[512]{0:T(512)S(1)} %add_rsqrt_fusion, f32[512]{0:T(512)S(1)} %broadcast_multiply_fusion), kind=kOutput, calls=%fused_computation.19 | convolution fusion | flops 5038407680 | bytes 15082496 | tf_op jit(solution)/shard_map/dot_general | solution.py:81
  144.0 6.3 %copy.10 = bf16[512,3840]{0,1:T(8,128)(2,1)} copy(bf16[512,3840]{1,0:T(8,128)(2,1)} %convolution_convert_fusion) | data formatting | bytes 7864320 | tf_op jit(solution)/shard_map/convert_element_type | solution.py:84
  150.3 1.9 slice.17
  152.2 2.5 collective-permute-start.1
  154.7 3.4 collective-permute-start
  158.7 2.5 slice_bitcast_fusion.2
  161.2 51.9 %collective-permute-done.1 = bf16[1,512,2,16,80]{1,4,3,2,0:T(8,128)(2,1)} collective-permute-done((bf16[1,512,2,16,80]{1,4,3,2,0:T(8,128)(2,1)S(1)}, bf16[1,512,2,16,80]{1,4,3,2,0:T(8,128)(2,1)}, u32[]{:S(2)}, u32[]{:S(2)}) %collective-permute-start.1) | collective-permute-done | bytes 2621472 | tf_op jit(solution)/shard_map/ppermute | solution.py:18
  213.0 28.8 %collective-permute-done = bf16[1,512,2,16,80]{1,4,3,2,0:T(8,128)(2,1)} collective-permute-done((bf16[1,512,2,16,80]{1,4,3,2,0:T(8,128)(2,1)S(1)}, bf16[1,512,2,16,80]{1,4,3,2,0:T(8,128)(2,1)}, u32[]{:S(2)}, u32[]{:S(2)}) %collective-permute-start) | collective-permute-done | bytes 2621472 | tf_op jit(solution)/shard_map/ppermute | solution.py:15
  241.8 3.4 pad_maximum_fusion
  245.3 3.4 slice_bitcast_fusion
  248.6 106.8 %while.18 = (s32[]{:T(128)}, bf16[16,512,80]{1,2,0:T(8,128)(2,1)S(1)}, s32[16]{0:T(128)S(1)}, bf16[512,16,80]{0,2,1:T(8,128)(2,1)}, bf16[1536,16,80]{0,2,1:T(8,1...) while((s32[]{:T(128)}, ...), condition=%wide.region_8.9_spmd.clone, body=%wide.region_5.8_spmd.clone.sunk | while | flops 258776064 | bytes 10112171 | solution.py:57
  251.2 1.7 fusion.38
  253.5 1.8 fusion.40
  257.8 1.8 fusion.38
  260.2 1.8 fusion.40
  264.5 1.8 fusion.38
  266.8 1.8 fusion.40
  271.2 1.8 fusion.38
  273.5 1.8 fusion.40
  277.9 1.8 fusion.38
  280.2 1.8 fusion.40
  284.5 1.8 fusion.38
  286.9 1.8 fusion.40
  291.2 1.8 fusion.38
  293.6 1.8 fusion.40
  297.9 1.8 fusion.38
  300.2 1.8 fusion.40
  304.6 1.8 fusion.38
  306.9 1.8 fusion.40
  311.3 1.8 fusion.38
  313.6 1.8 fusion.40
  317.9 1.8 fusion.38
  320.3 1.8 fusion.40
  324.6 1.8 fusion.38
  326.9 1.8 fusion.40
  331.3 1.8 fusion.38
  333.6 1.8 fusion.40
  338.0 1.8 fusion.38
  340.3 1.8 fusion.40
  344.6 1.8 fusion.38
  347.0 1.8 fusion.40
  351.3 1.8 fusion.38
  353.7 1.8 fusion.40
  356.5 4.2 fusion.18
  360.8 1.1 convolution_bitcast_fusion.1
  361.9 120.9 %all-reduce.2.cloned.1.call-done = f32[1,64,1280]{2,1,0:T(8,128)} async-done(((f32[1,64,1280]{2,1,0:T(8,128)}), f32[1,64,1280]{2,1,0:T(8,128)}) %all-reduce.2.cloned.1.call-update) | async-done | bytes 327696 | tf_op jit(solution)/shard_map/psum | solution.py:109
  482.9 1.8 broadcast_divide_fusion
  (67 shorter events, 22.2 us)
Async XLA Ops:
  7.2 1.3 copy-start
  7.2 125.9 %copy-start.4 = (f32[1280]{0:T(1024)S(1)}, f32[1280]{0:T(1024)}, u32[]{:S(2)}) copy-start(f32[1280]{0:T(1024)} %param.9) | copy-start | bytes 15364
  7.2 125.9 %all-gather.3.cloned.1.call-start = ((), (), s32[]{:S(2)}) async-start(), calls=%async_computation | async-start | bytes 14745600 | tf_op jit(solution)/shard_map/all_gather | solution.py:66
  7.9 347.6 %all-gather.5.cloned.1.call-start = ((), (), s32[]{:S(2)}) async-start(), calls=%async_computation.1 | async-start | bytes 4915200 | tf_op jit(solution)/shard_map/all_gather | solution.py:67
  150.3 7.9 %copy-start.3 = (s32[1,64]{1,0:T(1,128)S(1)}, s32[1,64]{1,0:T(1,128)}, u32[]{:S(2)}) copy-start(s32[1,64]{1,0:T(1,128)} %param.8) | copy-start | bytes 772
  152.2 60.8 %collective-permute-start.1 = (bf16[1,512,2,16,80]{1,4,3,2,0:T(8,128)(2,1)S(1)}, bf16[1,512,2,16,80]{1,4,3,2,0:T(8,128)(2,1)}, u32[]{:S(2)}, u32[]{:S(2)}) collective-permute-start(bf16[1,512,2,16,80]{1,4,3,2,0:T(8,128)(2,1)S(1)} %slice.17), channel_id=1, source_target_pairs={{2,0},{4,2},{6,4},{8,6},{10,8},{12,10},{14,12},{16,14},{18,16},{20... | collective-permute-start | bytes 7864328 | tf_op jit(solution)/shard_map/ppermute | solution.py:18
  154.7 87.1 %collective-permute-start = (bf16[1,512,2,16,80]{1,4,3,2,0:T(8,128)(2,1)S(1)}, bf16[1,512,2,16,80]{1,4,3,2,0:T(8,128)(2,1)}, u32[]{:S(2)}, u32[]{:S(2)}) collective-permute-start(bf16[1,512,2,16,80]{1,4,3,2,0:T(8,128)(2,1)S(1)} %slice.17), channel_id=1, source_target_pairs={{0,2},{2,4},{4,6},{6,8},{8,10},{10,12},{12,14},{14,16},{16,18},{18... | collective-permute-start | bytes 7864328 | tf_op jit(solution)/shard_map/ppermute | solution.py:15
  158.1 324.8 %all-reduce.2.cloned.1.call-start = ((), (), s32[]{:S(2)}) async-start(), calls=%async_computation.2 | async-start | bytes 655360 | tf_op jit(solution)/shard_map/psum | solution.py:109
  245.2 3.4 copy-start.5
  248.6 107.9 %copy-start.1 = (bf16[1,512,1280]{2,1,0:T(8,128)(2,1)S(1)}, bf16[1,512,1280]{2,1,0:T(8,128)(2,1)}, u32[]{:S(2)}) copy-start(bf16[1,512,1280]{2,1,0:T(8,128)(2,1)} %param.7) | copy-start | bytes 3932164
  355.5 1.1 copy-start.6
  360.8 123.9 %copy-start.2 = (bf16[1,512,1280]{2,1,0:T(8,128)(2,1)}, bf16[1,512,1280]{2,1,0:T(8,128)(2,1)S(1)}, u32[]{:S(2)}) copy-start(bf16[1,512,1280]{2,1,0:T(8,128)(2,1)S(1)} %fusion.18) | copy-start | bytes 3932164
Sparse Core Ops, SparseCore 0:
  9.6 123.4 all-gather.2
  158.2 47.8 all-gather.4
  362.1 120.7 all-reduce.1
where the time goes:
time: 493 us; the launch traced here: 491 us
  waiting for transfers between devices  326 us (66%)
  matrix products  73.3 us (15%)
  loops' own time  31.3 us (6%)
  local copies, waits for them, and re-layouts  25 us (5%)
  other arithmetic  15.6 us (3%)
  between operations  13.9 us (3%)
  starting transfers between devices  5.96 us (1%)
    all_gather x1, waiting for transfers between devices, shards(): lax.all_gather(w_qkv, 'dp', axis=0, tiled=True)  124 us
    psum x1, waiting for transfers between devices, shards(): sums = lax.psum(terms, ('sx', 'sy'))  121 us
    ppermute x1, waiting for transfers between devices, with_halo(): lax.ppermute(lax.slice_in_dim(block, 0, width, axis=dim), axis, backward)  51.9 us
    another operation x1, loops' own time, one_block(): outcome = lax.map(one_head, jnp.arange(heads, dtype=jnp.int32))  31.3 us
    dot_general x16, matrix products, one_head(): jnp.dot(probs, v_head, preferred_element_type=jnp.float32)  28.9 us
    ppermute x1, waiting for transfers between devices, with_halo(): lax.ppermute(lax.slice_in_dim(block, block.shape[dim] - width, None, axis...  28.8 us
    dot_general x16, matrix products, one_head(): jnp.dot(q_head, k_head.T, preferred_element_type=jnp.float32) * scale  28.1 us
    dot_general x1, matrix products, shards(): jnp.dot(normed.reshape(count_rows * local, width), qkv_full, preferred_el...  10.9 us
  transfers between devices with their start and end apart: 5, of which 4 were waited for; matrix products, arithmetic and copies ran while one was open for 18% of the time, Pallas kernels for 0%

commit v1 on v0

--- a/solution.py
+++ b/solution.py
@@ -1,3 +1,4 @@
+import functools
 import jax
 import jax.numpy as jnp
 from jax import lax
@@ -5,6 +6,13 @@
 
 HEADS = 16
 MAXLEN = 512
+
+
+def fit_panel(obj, axis_key):
+    return lax.all_gather(obj, axis_key).sum(axis=0)
+
+
+extend_records = functools.partial(fit_panel, axis_key=("sx", "sy"))
 
 
 def with_halo(block, sides, width):
@@ -106,7 +114,7 @@
     onehot = (labels[:, None] == own_list[rowidx][None, :]).astype(jnp.bfloat16)
     parts_list = [jnp.dot(onehot, hidden[rowidx], preferred_element_type=jnp.float32)]
     terms = jnp.stack(parts_list, axis=0)
-    sums = lax.psum(terms, ("sx", "sy"))
+    sums = extend_records(terms)
     pooled = sums / lengths.astype(jnp.float32)[:, :, None]
     return (hidden, pooled)
 

time: 493 us -> 461 us (0.935)
  waiting for transfers between devices: 326 us -> 291 us
    psum x1 -> x0, waiting for transfers between devices: 121 us -> none  [shards(): sums = lax.psum(terms, ('sx', 'sy'))]
    all_gather x0 -> x1, waiting for transfers between devices: none -> 85.4 us  [fit_panel(): return lax.all_gather(obj, axis_key).sum(axis=0)]
  transfers between devices with their start and end apart: 5 -> 5, of which waited for: 4 -> 4; matrix products, arithmetic and copies ran while one was open for 18% -> 19% of each run, Pallas kernels for 0% -> 0%
where the time goes in v1:
time: 461 us; the launch traced here: 457 us
  waiting for transfers between devices  291 us (63%)
  matrix products  73.3 us (16%)
  loops' own time  31.3 us (7%)
  local copies, waits for them, and re-layouts  25 us (5%)
  other arithmetic  17.4 us (4%)
  between operations  13.9 us (3%)
  starting transfers between devices  5.96 us (1%)
    all_gather x1, waiting for transfers between devices, shards(): lax.all_gather(w_qkv, 'dp', axis=0, tiled=True)  124 us
    all_gather x1, waiting for transfers between devices, fit_panel(): return lax.all_gather(obj, axis_key).sum(axis=0)  85.4 us
    ppermute x1, waiting for transfers between devices, with_halo(): lax.ppermute(lax.slice_in_dim(block, 0, width, axis=dim), axis, backward)  51.9 us
    another operation x1, loops' own time, one_block(): outcome = lax.map(one_head, jnp.arange(heads, dtype=jnp.int32))  31.3 us
    dot_general x16, matrix products, one_head(): jnp.dot(probs, v_head, preferred_element_type=jnp.float32)  28.9 us
    ppermute x1, waiting for transfers between devices, with_halo(): lax.ppermute(lax.slice_in_dim(block, block.shape[dim] - width, None, axis...  28.8 us
    dot_general x16, matrix products, one_head(): jnp.dot(q_head, k_head.T, preferred_element_type=jnp.float32) * scale  28.1 us
    dot_general x1, matrix products, shards(): jnp.dot(normed.reshape(count_rows * local, width), qkv_full, preferred_el...  10.9 us
  transfers between devices with their start and end apart: 5, of which 4 were waited for; matrix products, arithmetic and copies ran while one was open for 19% of the time, Pallas kernels for 0%

profile of v1, /device:TPU:8, one launch (start us, length us, event | category | flops | bytes accessed | tf_op | source)
XLA Modules:
  0.0 457.4 jit_solution(18438258062931336821)
XLA Ops:
  9.2 123.8 %all-gather.5.cloned.1.call-done = bf16[1280,3840]{1,0:T(8,128)(2,1)} async-done(((bf16[640,3840]{1,0:T(8,128)(2,1)}), bf16[1280,3840]{1,0:T(8,128)(2,1)}) %all-gather.5.cloned.1.call-update) | async-done | bytes 9830416 | tf_op jit(solution)/shard_map/all_gather | solution.py:74
  133.0 10.9 %convolution_convert_fusion = bf16[512,3840]{1,0:T(8,128)(2,1)} fusion(bf16[1280,3840]{1,0:T(8,128)(2,1)} %all-gather.5.cloned.1.call-done, bf16[1,512,1280]{2,1,0:T(8,128)(2,1)S(1)} %copy-done, f32[1280]{0:T(1024)S(1)} %copy-done.4, f32[512]{0:T(512)S(1)} %add_rsqrt_fusion, f32[512]{0:T(512)S(1)} %broadcast_multiply_fusion), kind=kOutput, calls=%fused_computation.19 | convolution fusion | flops 5038407680 | bytes 15082496 | tf_op jit(solution)/shard_map/dot_general | solution.py:89
  144.0 6.3 %copy.10 = bf16[512,3840]{0,1:T(8,128)(2,1)} copy(bf16[512,3840]{1,0:T(8,128)(2,1)} %convolution_convert_fusion) | data formatting | bytes 7864320 | tf_op jit(solution)/shard_map/convert_element_type | solution.py:92
  150.3 1.9 slice.17
  152.2 2.5 collective-permute-start.1
  154.7 3.4 collective-permute-start
  158.7 2.5 slice_bitcast_fusion.2
  161.2 51.9 %collective-permute-done.1 = bf16[1,512,2,16,80]{1,4,3,2,0:T(8,128)(2,1)} collective-permute-done((bf16[1,512,2,16,80]{1,4,3,2,0:T(8,128)(2,1)S(1)}, bf16[1,512,2,16,80]{1,4,3,2,0:T(8,128)(2,1)}, u32[]{:S(2)}, u32[]{:S(2)}) %collective-permute-start.1) | collective-permute-done | bytes 2621472 | tf_op jit(solution)/shard_map/ppermute | solution.py:26
  213.0 28.8 %collective-permute-done = bf16[1,512,2,16,80]{1,4,3,2,0:T(8,128)(2,1)} collective-permute-done((bf16[1,512,2,16,80]{1,4,3,2,0:T(8,128)(2,1)S(1)}, bf16[1,512,2,16,80]{1,4,3,2,0:T(8,128)(2,1)}, u32[]{:S(2)}, u32[]{:S(2)}) %collective-permute-start) | collective-permute-done | bytes 2621472 | tf_op jit(solution)/shard_map/ppermute | solution.py:23
  241.8 3.4 pad_maximum_fusion
  245.3 3.4 slice_bitcast_fusion
  248.6 106.8 %while.18 = (s32[]{:T(128)}, bf16[16,512,80]{1,2,0:T(8,128)(2,1)S(1)}, s32[16]{0:T(128)S(1)}, bf16[512,16,80]{0,2,1:T(8,128)(2,1)}, bf16[1536,16,80]{0,2,1:T(8,1...) while((s32[]{:T(128)}, ...), condition=%wide.region_8.9_spmd.clone, body=%wide.region_5.8_spmd.clone.sunk | while | flops 258776064 | bytes 10112171 | solution.py:65
  251.2 1.7 fusion.39
  253.5 1.8 fusion.41
  257.8 1.8 fusion.39
  260.2 1.8 fusion.41
  264.5 1.8 fusion.39
  266.8 1.8 fusion.41
  271.2 1.8 fusion.39
  273.5 1.8 fusion.41
  277.9 1.8 fusion.39
  280.2 1.8 fusion.41
  284.5 1.8 fusion.39
  286.9 1.8 fusion.41
  291.2 1.8 fusion.39
  293.6 1.8 fusion.41
  297.9 1.8 fusion.39
  300.2 1.8 fusion.41
  304.6 1.8 fusion.39
  306.9 1.8 fusion.41
  311.3 1.8 fusion.39
  313.6 1.8 fusion.41
  317.9 1.8 fusion.39
  320.3 1.8 fusion.41
  324.6 1.8 fusion.39
  326.9 1.8 fusion.41
  331.3 1.8 fusion.39
  333.6 1.8 fusion.41
  338.0 1.8 fusion.39
  340.3 1.8 fusion.41
  344.6 1.8 fusion.39
  347.0 1.8 fusion.41
  351.3 1.8 fusion.39
  353.7 1.8 fusion.41
  356.5 4.2 fusion.18
  360.8 1.1 fusion.24
  361.9 85.4 %all-gather.9.cloned.1.call-done = f32[1024,1280]{1,0:T(8,128)} async-done(((f32[64,1280]{1,0:T(8,128)}), f32[1024,1280]{1,0:T(8,128)}) %all-gather.9.cloned.1.call-update) | async-done | bytes 5242896 | tf_op jit(solution)/shard_map/all_gather | solution.py:12
  447.3 2.8 reduce.3
  (68 shorter events, 23.0 us)
Async XLA Ops:
  7.2 1.3 copy-start
  7.2 125.9 %copy-start.4 = (f32[1280]{0:T(1024)S(1)}, f32[1280]{0:T(1024)}, u32[]{:S(2)}) copy-start(f32[1280]{0:T(1024)} %param.9) | copy-start | bytes 15364
  7.2 125.9 %all-gather.5.cloned.1.call-start = ((), (), s32[]{:S(2)}) async-start(), calls=%async_computation | async-start | bytes 14745600 | tf_op jit(solution)/shard_map/all_gather | solution.py:74
  7.9 347.6 %all-gather.7.cloned.1.call-start = ((), (), s32[]{:S(2)}) async-start(), calls=%async_computation.1 | async-start | bytes 4915200 | tf_op jit(solution)/shard_map/all_gather | solution.py:75
  150.3 7.9 %copy-start.3 = (s32[1,64]{1,0:T(1,128)S(1)}, s32[1,64]{1,0:T(1,128)}, u32[]{:S(2)}) copy-start(s32[1,64]{1,0:T(1,128)} %param.8) | copy-start | bytes 772
  152.2 60.8 %collective-permute-start.1 = (bf16[1,512,2,16,80]{1,4,3,2,0:T(8,128)(2,1)S(1)}, bf16[1,512,2,16,80]{1,4,3,2,0:T(8,128)(2,1)}, u32[]{:S(2)}, u32[]{:S(2)}) collective-permute-start(bf16[1,512,2,16,80]{1,4,3,2,0:T(8,128)(2,1)S(1)} %slice.17), channel_id=1, source_target_pairs={{2,0},{4,2},{6,4},{8,6},{10,8},{12,10},{14,12},{16,14},{18,16},{20... | collective-permute-start | bytes 7864328 | tf_op jit(solution)/shard_map/ppermute | solution.py:26
  154.7 87.1 %collective-permute-start = (bf16[1,512,2,16,80]{1,4,3,2,0:T(8,128)(2,1)S(1)}, bf16[1,512,2,16,80]{1,4,3,2,0:T(8,128)(2,1)}, u32[]{:S(2)}, u32[]{:S(2)}) collective-permute-start(bf16[1,512,2,16,80]{1,4,3,2,0:T(8,128)(2,1)S(1)} %slice.17), channel_id=1, source_target_pairs={{0,2},{2,4},{4,6},{6,8},{8,10},{10,12},{12,14},{14,16},{16,18},{18... | collective-permute-start | bytes 7864328 | tf_op jit(solution)/shard_map/ppermute | solution.py:23
  158.1 289.2 %all-gather.9.cloned.1.call-start = ((), (), s32[]{:S(2)}) async-start(), calls=%async_computation.2 | async-start | bytes 5570560 | tf_op jit(solution)/shard_map/all_gather | solution.py:12
  245.2 3.4 copy-start.5
  248.6 107.9 %copy-start.1 = (bf16[1,512,1280]{2,1,0:T(8,128)(2,1)S(1)}, bf16[1,512,1280]{2,1,0:T(8,128)(2,1)}, u32[]{:S(2)}) copy-start(bf16[1,512,1280]{2,1,0:T(8,128)(2,1)} %param.7) | copy-start | bytes 3932164
  355.5 1.1 copy-start.6
  360.8 89.3 %copy-start.2 = (bf16[1,512,1280]{2,1,0:T(8,128)(2,1)}, bf16[1,512,1280]{2,1,0:T(8,128)(2,1)S(1)}, u32[]{:S(2)}) copy-start(bf16[1,512,1280]{2,1,0:T(8,128)(2,1)S(1)} %fusion.18) | copy-start | bytes 3932164
Sparse Core Ops, SparseCore 0:
  9.6 123.4 all-gather.4
  158.2 47.8 all-gather.6
  362.1 85.2 all-gather.8
